TPU v7x, 32 devices: a whole 2x2x4 slice. The times are simulated.
32 devices in a mesh: seq: 8 (over z, y), head: 4 (over x, core).
Axes of the slice: x: 2, y: 2, z: 4, core: 2. Of those that a mesh axis runs over, the one named last changes fastest.
Arguments:
- tail_queries: bfloat16 [10, 64, 4096], P(None, 'seq', 'head'), may hold values from -8 to 8
- keys: bfloat16 [10, 16384, 1024], P(None, 'seq', 'head'), may hold values from -160 to 160
Outputs:
- vertical: float32 [10, 32, 16384], P(None, 'head', 'seq')
- slash: float32 [10, 32, 16384], P(None, 'head', 'seq')
All inputs are finite; a program needn't handle non-finite values.
Results may differ from a plain program's by a relative error of at most 0.0003.
Values may be sent and summed in bfloat16 or wider, within the bound.
A program may use at most 64 MiB of HBM per device.

v0:
```python
import math

import jax
import jax.numpy as jnp
from jax import lax
from jax.sharding import PartitionSpec as P

HD = 128
LAST = 64


def from_behind(value, axis, steps):
    count = lax.axis_size(axis)
    initial, last = (max(0, -steps), min(count, count - steps))
    return lax.ppermute(value, axis, [(source, source + steps) for source in range(initial, last)])


def diagonal_sums(probabilities):
    head_count, query_count, key_count = probabilities.shape
    width = key_count + (query_count + 127) // 128 * 128
    rows = jnp.pad(probabilities[:, ::-1, :], ((0, 0), (0, 0), (0, width - key_count)))
    offset = 1
    while rows.shape[1] > 1:
        even_rows = rows[:, 0::2, :]
        odd_rows = rows[:, 1::2, :]
        odd_rows = jnp.pad(odd_rows[:, :, : width - offset], ((0, 0), (0, 0), (offset, 0)))
        rows = even_rows + odd_rows
        offset = offset * 2
    return rows[:, 0, : key_count + query_count]


def local_scores(queries, layer_keys):
    seq_count = lax.axis_size("seq")
    shard_index = lax.axis_index("seq")
    key_count = layer_keys.shape[0]
    groups = layer_keys.shape[1] // HD
    head_count = queries.shape[1] // HD
    per_group = head_count // groups
    tokens = key_count * seq_count
    grouped_queries = queries.reshape(LAST, groups, per_group, HD)
    grouped_keys = layer_keys.reshape(key_count, groups, HD)
    scores = jnp.einsum(
        "qgad,kgd->gaqk", grouped_queries, grouped_keys, preferred_element_type=jnp.float32
    )
    scores = scores.reshape(head_count, LAST, key_count) * (1.0 / math.sqrt(HD))
    positions = tokens - LAST + lax.iota(jnp.int32, LAST)
    key_positions = shard_index * key_count + lax.iota(jnp.int32, key_count)
    visible = key_positions[None, :] <= positions[:, None]
    return jnp.where(visible[None], scores, -jnp.inf)


def local_stats(scores):
    local_max = jnp.max(scores, axis=2)
    weights = jnp.exp(scores - local_max[:, :, None])
    return (local_max, weights, jnp.sum(weights, axis=2))


def spread(weights, local_max, row_max, row_total):
    factor = jnp.exp(local_max - row_max) / row_total
    probabilities = weights * factor[:, :, None]
    return (jnp.sum(probabilities, axis=1), diagonal_sums(probabilities))


def stats_every(local_max, local_total):
    row_max = lax.pmax(local_max, "seq")
    row_total = lax.psum(local_total * jnp.exp(local_max - row_max), "seq")
    return (row_max, row_total)


def on_device(tail_queries, keys):
    gathered = lax.all_gather(tail_queries, "seq", axis=1, tiled=True)
    key_count = keys.shape[1]
    ratio = key_count * lax.axis_size("seq") / LAST

    def first_pass(inputs):
        local_max, weights, local_total = local_stats(local_scores(inputs[0], inputs[1]))
        return (local_max, local_total, weights[:, :, key_count - LAST :])

    local_max, local_total, blocks = lax.map(first_pass, (gathered, keys))
    row_max, row_total = stats_every(local_max, local_total)

    def second_pass(inputs):
        layer_max, weights, unused = local_stats(local_scores(inputs[0], inputs[1]))
        return spread(weights, layer_max, inputs[2], inputs[3])

    vertical, skewed = lax.map(second_pass, (gathered, keys, row_max, row_total))
    overflow = from_behind(skewed[:, :, key_count:], "seq", 1)
    slash = skewed[:, :, :key_count].at[:, :, :LAST].add(overflow) * ratio
    return (vertical * ratio, slash)


def solution(mesh):
    return jax.shard_map(
        on_device,
        mesh=mesh,
        in_specs=(P(None, "seq", "head"), P(None, "seq", "head")),
        out_specs=(P(None, "head", "seq"), P(None, "head", "seq")),
        check_vma=False,
    )
```

profile of v0, /device:TPU:0, one launch (start us, length us, event | category | flops | bytes accessed | tf_op | source)
XLA Modules:
  0.0 723.6 jit_solution(18158448952666337772)
XLA Ops:
  7.9 14.2 %copy.12 = bf16[10,2048,256]{1,2,0:T(8,128)(2,1)} copy(bf16[10,2048,256]{2,1,0:T(8,128)(2,1)} %param.9) | data formatting | bytes 20971520 | tf_op jit(solution)/shard_map/while | solution.py:86
  22.2 32.5 %all-gather.2.cloned.1.call-done = bf16[10,64,1024]{2,1,0:T(8,128)(2,1)} async-done(((bf16[10,8,1024]{2,1,0:T(8,128)(2,1)}), bf16[10,64,1024]{2,1,0:T(8,128)(2,1)}) %all-gather.2.cloned.1.call-update) | async-done | bytes 1310736 | tf_op jit(solution)/shard_map/all_gather | solution.py:71
  54.7 44.8 %while.27 = (s32[]{:T(128)}, f32[10,8,64]{2,1,0:T(8,128)S(1)}, f32[10,8,64]{2,1,0:T(8,128)S(1)}, bf16[10,2048,256]{1,2,0:T(8,128)(2,1)}, bf16[10,64,1024]{2,1,0:...) while((s32[]{:T(128)}, f32[10,8,64]{2,1,0:T(8,128)S(1)}, f32[10,8,64]{2,1,0:T(8,128)S(1)}, ...), condition=%wide.region_3.4_spmd, body=%wide.region_0.3_spmd.sunk | while | flops 275907648 | bytes 12622497 | solution.py:79
  99.6 35.4 %pmax.7 = f32[10,8,64]{2,1,0:T(8,128)S(1)} all-reduce(f32[10,8,64]{2,1,0:T(8,128)S(1)} %get-tuple-element.132), channel_id=1, replica_groups=mesh['seq'=8,'head'=4] {'seq'}, use_global_device_ids=true, to_apply=%region_4.5 | all-reduce | flops 5120 | bytes 40960 | tf_op jit(solution)/shard_map/pmax | solution.py:65
  135.0 33.4 %psum.7 = f32[10,8,64]{2,1,0:T(8,128)S(1)} all-reduce(f32[10,8,64]{2,1,0:T(8,128)S(1)} %exponential_multiply_fusion), channel_id=1, replica_groups=mesh['seq'=8,'head'=4] {'seq'}, use_global_device_ids=true, to_apply=%region_5.6 | all-reduce | flops 5120 | bytes 40960 | tf_op jit(solution)/shard_map/psum | solution.py:66
  168.3 541.3 %while.28 = (s32[]{:T(128)}, f32[10,8,2048]{2,1,0:T(8,128)}, f32[10,8,2112]{2,1,0:T(8,128)}, bf16[10,2048,256]{1,2,0:T(8,128)(2,1)}, bf16[10,64,1024]{2,1,0:T(8,...) while((s32[]{:T(128)}, f32[10,8,2048]{2,1,0:T(8,128)}, ...), condition=%wide.region_9.10_spmd, body=%wide.region_6.9_spmd.sunk | while | flops 280135744 | bytes 69350088 | solution.py:86
  175.8 10.2 %rev.7 = f32[8,64,2048]{2,1,0:T(8,128)} reverse(f32[8,64,2048]{2,1,0:T(8,128)} %fusion.22), dimensions={1} | reverse | bytes 8388608 | tf_op jit(solution)/shard_map/while/body/eval_jaxpr/rev | solution.py:21
  186.1 4.7 pad.73
  191.4 9.9 %slice.171 = f32[8,32,2176]{2,1,0:T(8,128)} slice(f32[8,64,2176]{2,1,0:T(8,128)} %pad.73), slice={[0:8:1], [1:64:2], [0:2176:1]} | slice | bytes 4456448 | tf_op jit(solution)/shard_map/while/body/eval_jaxpr/slice | solution.py:25
  201.3 9.9 %slice.170 = f32[8,32,2176]{2,1,0:T(8,128)} slice(f32[8,64,2176]{2,1,0:T(8,128)} %pad.73), slice={[0:8:1], [0:64:2], [0:2176:1]} | slice | bytes 4456448 | tf_op jit(solution)/shard_map/while/body/eval_jaxpr/slice | solution.py:24
  229.9 10.2 %rev.7 = f32[8,64,2048]{2,1,0:T(8,128)} reverse(f32[8,64,2048]{2,1,0:T(8,128)} %fusion.22), dimensions={1} | reverse | bytes 8388608 | tf_op jit(solution)/shard_map/while/body/eval_jaxpr/rev | solution.py:21
  240.2 4.7 pad.73
  245.6 9.9 %slice.171 = f32[8,32,2176]{2,1,0:T(8,128)} slice(f32[8,64,2176]{2,1,0:T(8,128)} %pad.73), slice={[0:8:1], [1:64:2], [0:2176:1]} | slice | bytes 4456448 | tf_op jit(solution)/shard_map/while/body/eval_jaxpr/slice | solution.py:25
  255.5 9.9 %slice.170 = f32[8,32,2176]{2,1,0:T(8,128)} slice(f32[8,64,2176]{2,1,0:T(8,128)} %pad.73), slice={[0:8:1], [0:64:2], [0:2176:1]} | slice | bytes 4456448 | tf_op jit(solution)/shard_map/while/body/eval_jaxpr/slice | solution.py:24
  284.1 10.2 %rev.7 = f32[8,64,2048]{2,1,0:T(8,128)} reverse(f32[8,64,2048]{2,1,0:T(8,128)} %fusion.22), dimensions={1} | reverse | bytes 8388608 | tf_op jit(solution)/shard_map/while/body/eval_jaxpr/rev | solution.py:21
  294.3 4.7 pad.73
  299.7 9.9 %slice.171 = f32[8,32,2176]{2,1,0:T(8,128)} slice(f32[8,64,2176]{2,1,0:T(8,128)} %pad.73), slice={[0:8:1], [1:64:2], [0:2176:1]} | slice | bytes 4456448 | tf_op jit(solution)/shard_map/while/body/eval_jaxpr/slice | solution.py:25
  309.6 9.9 %slice.170 = f32[8,32,2176]{2,1,0:T(8,128)} slice(f32[8,64,2176]{2,1,0:T(8,128)} %pad.73), slice={[0:8:1], [0:64:2], [0:2176:1]} | slice | bytes 4456448 | tf_op jit(solution)/shard_map/while/body/eval_jaxpr/slice | solution.py:24
  319.5 2.9 pad_add_fusion.11
  338.2 10.2 %rev.7 = f32[8,64,2048]{2,1,0:T(8,128)} reverse(f32[8,64,2048]{2,1,0:T(8,128)} %fusion.22), dimensions={1} | reverse | bytes 8388608 | tf_op jit(solution)/shard_map/while/body/eval_jaxpr/rev | solution.py:21
  348.5 4.7 pad.73
  353.8 9.9 %slice.171 = f32[8,32,2176]{2,1,0:T(8,128)} slice(f32[8,64,2176]{2,1,0:T(8,128)} %pad.73), slice={[0:8:1], [1:64:2], [0:2176:1]} | slice | bytes 4456448 | tf_op jit(solution)/shard_map/while/body/eval_jaxpr/slice | solution.py:25
  363.7 9.9 %slice.170 = f32[8,32,2176]{2,1,0:T(8,128)} slice(f32[8,64,2176]{2,1,0:T(8,128)} %pad.73), slice={[0:8:1], [0:64:2], [0:2176:1]} | slice | bytes 4456448 | tf_op jit(solution)/shard_map/while/body/eval_jaxpr/slice | solution.py:24
  392.3 10.2 %rev.7 = f32[8,64,2048]{2,1,0:T(8,128)} reverse(f32[8,64,2048]{2,1,0:T(8,128)} %fusion.22), dimensions={1} | reverse | bytes 8388608 | tf_op jit(solution)/shard_map/while/body/eval_jaxpr/rev | solution.py:21
  402.6 4.7 pad.73
  407.9 9.9 %slice.171 = f32[8,32,2176]{2,1,0:T(8,128)} slice(f32[8,64,2176]{2,1,0:T(8,128)} %pad.73), slice={[0:8:1], [1:64:2], [0:2176:1]} | slice | bytes 4456448 | tf_op jit(solution)/shard_map/while/body/eval_jaxpr/slice | solution.py:25
  417.8 9.9 %slice.170 = f32[8,32,2176]{2,1,0:T(8,128)} slice(f32[8,64,2176]{2,1,0:T(8,128)} %pad.73), slice={[0:8:1], [0:64:2], [0:2176:1]} | slice | bytes 4456448 | tf_op jit(solution)/shard_map/while/body/eval_jaxpr/slice | solution.py:24
  427.7 2.9 pad_add_fusion.11
  446.5 10.2 %rev.7 = f32[8,64,2048]{2,1,0:T(8,128)} reverse(f32[8,64,2048]{2,1,0:T(8,128)} %fusion.22), dimensions={1} | reverse | bytes 8388608 | tf_op jit(solution)/shard_map/while/body/eval_jaxpr/rev | solution.py:21
  456.7 4.7 pad.73
  462.1 9.9 %slice.171 = f32[8,32,2176]{2,1,0:T(8,128)} slice(f32[8,64,2176]{2,1,0:T(8,128)} %pad.73), slice={[0:8:1], [1:64:2], [0:2176:1]} | slice | bytes 4456448 | tf_op jit(solution)/shard_map/while/body/eval_jaxpr/slice | solution.py:25
  472.0 9.9 %slice.170 = f32[8,32,2176]{2,1,0:T(8,128)} slice(f32[8,64,2176]{2,1,0:T(8,128)} %pad.73), slice={[0:8:1], [0:64:2], [0:2176:1]} | slice | bytes 4456448 | tf_op jit(solution)/shard_map/while/body/eval_jaxpr/slice | solution.py:24
  500.6 10.2 %rev.7 = f32[8,64,2048]{2,1,0:T(8,128)} reverse(f32[8,64,2048]{2,1,0:T(8,128)} %fusion.22), dimensions={1} | reverse | bytes 8388608 | tf_op jit(solution)/shard_map/while/body/eval_jaxpr/rev | solution.py:21
  510.9 4.7 pad.73
  516.2 9.9 %slice.171 = f32[8,32,2176]{2,1,0:T(8,128)} slice(f32[8,64,2176]{2,1,0:T(8,128)} %pad.73), slice={[0:8:1], [1:64:2], [0:2176:1]} | slice | bytes 4456448 | tf_op jit(solution)/shard_map/while/body/eval_jaxpr/slice | solution.py:25
  526.1 9.9 %slice.170 = f32[8,32,2176]{2,1,0:T(8,128)} slice(f32[8,64,2176]{2,1,0:T(8,128)} %pad.73), slice={[0:8:1], [0:64:2], [0:2176:1]} | slice | bytes 4456448 | tf_op jit(solution)/shard_map/while/body/eval_jaxpr/slice | solution.py:24
  554.7 10.2 %rev.7 = f32[8,64,2048]{2,1,0:T(8,128)} reverse(f32[8,64,2048]{2,1,0:T(8,128)} %fusion.22), dimensions={1} | reverse | bytes 8388608 | tf_op jit(solution)/shard_map/while/body/eval_jaxpr/rev | solution.py:21
  565.0 4.7 pad.73
  570.3 9.9 %slice.171 = f32[8,32,2176]{2,1,0:T(8,128)} slice(f32[8,64,2176]{2,1,0:T(8,128)} %pad.73), slice={[0:8:1], [1:64:2], [0:2176:1]} | slice | bytes 4456448 | tf_op jit(solution)/shard_map/while/body/eval_jaxpr/slice | solution.py:25
  580.2 9.9 %slice.170 = f32[8,32,2176]{2,1,0:T(8,128)} slice(f32[8,64,2176]{2,1,0:T(8,128)} %pad.73), slice={[0:8:1], [0:64:2], [0:2176:1]} | slice | bytes 4456448 | tf_op jit(solution)/shard_map/while/body/eval_jaxpr/slice | solution.py:24
  608.8 10.2 %rev.7 = f32[8,64,2048]{2,1,0:T(8,128)} reverse(f32[8,64,2048]{2,1,0:T(8,128)} %fusion.22), dimensions={1} | reverse | bytes 8388608 | tf_op jit(solution)/shard_map/while/body/eval_jaxpr/rev | solution.py:21
  619.1 4.7 pad.73
  624.4 9.9 %slice.171 = f32[8,32,2176]{2,1,0:T(8,128)} slice(f32[8,64,2176]{2,1,0:T(8,128)} %pad.73), slice={[0:8:1], [1:64:2], [0:2176:1]} | slice | bytes 4456448 | tf_op jit(solution)/shard_map/while/body/eval_jaxpr/slice | solution.py:25
  634.3 9.9 %slice.170 = f32[8,32,2176]{2,1,0:T(8,128)} slice(f32[8,64,2176]{2,1,0:T(8,128)} %pad.73), slice={[0:8:1], [0:64:2], [0:2176:1]} | slice | bytes 4456448 | tf_op jit(solution)/shard_map/while/body/eval_jaxpr/slice | solution.py:24
  662.9 10.2 %rev.7 = f32[8,64,2048]{2,1,0:T(8,128)} reverse(f32[8,64,2048]{2,1,0:T(8,128)} %fusion.22), dimensions={1} | reverse | bytes 8388608 | tf_op jit(solution)/shard_map/while/body/eval_jaxpr/rev | solution.py:21
  673.2 4.7 pad.73
  678.6 9.9 %slice.171 = f32[8,32,2176]{2,1,0:T(8,128)} slice(f32[8,64,2176]{2,1,0:T(8,128)} %pad.73), slice={[0:8:1], [1:64:2], [0:2176:1]} | slice | bytes 4456448 | tf_op jit(solution)/shard_map/while/body/eval_jaxpr/slice | solution.py:25
  688.5 9.9 %slice.170 = f32[8,32,2176]{2,1,0:T(8,128)} slice(f32[8,64,2176]{2,1,0:T(8,128)} %pad.73), slice={[0:8:1], [0:64:2], [0:2176:1]} | slice | bytes 4456448 | tf_op jit(solution)/shard_map/while/body/eval_jaxpr/slice | solution.py:24
  (403 shorter events, 239.0 us)
Async XLA Ops:
  7.2 47.6 %all-gather.2.cloned.1.call-start = ((), (), s32[]{:S(2)}) async-start(), calls=%async_computation | async-start | bytes 1474560 | tf_op jit(solution)/shard_map/all_gather | solution.py:71
  710.3 4.4 collective-permute-start
Sparse Core Ops, SparseCore 0:
  10.2 44.5 all-gather.1
where the time goes:
time: 733 us; the launch traced here: 724 us
  local copies, waits for them, and re-layouts  474 us (65%)
  other arithmetic  113 us (15%)
  blocking collectives  68.7 us (9%)
  waiting for transfers between devices  33.2 us (5%)
  matrix products  18.1 us (2%)
  between operations  14.1 us (2%)
    slice x60, local copies, waits for them, and re-layouts, diagonal_sums(): even_rows = rows[:, 0::2, :]  136 us
    slice x50, local copies, waits for them, and re-layouts, diagonal_sums(): odd_rows = rows[:, 1::2, :]  112 us
    rev x10, local copies, waits for them, and re-layouts, diagonal_sums(): probabilities[:, ::-1, :]  102 us
    add x50, other arithmetic, diagonal_sums(): rows = even_rows + odd_rows  51.7 us
    pad x10, local copies, waits for them, and re-layouts, diagonal_sums(): jnp.pad(probabilities[:, ::-1, :], ((0, 0), (0, 0), (0, width - key_count)))  47.2 us
    dynamic_slice x40, local copies, waits for them, and re-layouts, on_device(): local_max, local_total, blocks = lax.map(first_pass, (gathered, keys))  44.4 us
    pmax x1, blocking collectives, stats_every(): row_max = lax.pmax(local_max, 'seq')  35.4 us
    psum x1, blocking collectives, stats_every(): row_total = lax.psum(local_total * jnp.exp(local_max - row_max), 'seq')  33.4 us
  transfers between devices with their start and end apart: 2, of which 1 were waited for; matrix products, arithmetic and copies ran while one was open for 2% of the time, Pallas kernels for 0%

commit v1 on v0

v1 whole, which is shorter than its diff:
```python
import functools
import math

import jax
import jax.numpy as jnp
from jax import lax
from jax.experimental import pallas as pl
from jax.experimental.pallas import tpu as pltpu
from jax.sharding import PartitionSpec as P

HD = 128
LAST = 64
LANES = 128
LAG = 4
KEY_SLOTS = 3
BLOCK = 8
SCORE_COLUMNS = 512


def kernel(
    n, fast, q_ref, k_ref, vert_ref, slash_ref,
    qg, kbuf, w, st_tx, st_rx, ov_tx, ov_rx,
    own_sem, k_sem, zs, zr, ys, yr, ss, sr, osem, orsem,
):
    layers, rows, _ = q_ref.shape
    key_count = k_ref.shape[1]
    groups = k_ref.shape[2] // HD
    heads = rows * n // LAST
    per_group = heads // groups
    tiles = key_count // LANES
    slow = n // fast
    slots = LAG + 1
    tokens = key_count * n
    scale = math.log2(math.e) / math.sqrt(HD)
    ratio = tokens / LAST

    me = lax.axis_index("seq")
    my_slow = lax.div(me, fast)
    my_fast = lax.rem(me, fast)
    lane = lax.broadcasted_iota(jnp.int32, (heads, LANES), 1)

    def remote(src, dst, send, recv, dest):
        return pltpu.make_async_remote_copy(
            src_ref=src, dst_ref=dst, send_sem=send, recv_sem=recv,
            device_id={"seq": dest}, device_id_type=pl.DeviceIdType.MESH,
        )

    def wait_for(ref, sem):
        pltpu.make_async_copy(ref, ref, sem).wait()

    def key_copy(layer):
        slot = lax.rem(layer, KEY_SLOTS)
        return pltpu.make_async_copy(k_ref.at[layer], kbuf.at[slot], k_sem.at[slot])

    for layer in range(min(KEY_SLOTS - 1, layers)):
        key_copy(jnp.int32(layer)).start()
    own_copy = pltpu.make_async_copy(q_ref, qg.at[:, me], own_sem)
    own_copy.start()

    barrier = pltpu.get_barrier_semaphore()
    for d in range(1, n):
        pl.semaphore_signal(
            barrier, inc=1, device_id={"seq": lax.rem(me + d, n)},
            device_id_type=pl.DeviceIdType.MESH,
        )
    pl.semaphore_wait(barrier, n - 1)

    partner = my_slow * fast + lax.rem(my_fast + 1, fast)

    def send_queries(layer, carry):
        for d in range(1, slow):
            dest = lax.rem(my_slow + d, slow) * fast + my_fast
            remote(q_ref.at[layer], qg.at[layer, me], zs.at[layer], zr.at[layer], dest).start()
        if fast > 1:
            remote(q_ref.at[layer], qg.at[layer, me], ys.at[layer], yr.at[layer], partner).start()
        return carry

    lax.fori_loop(0, layers, send_queries, 0)

    def forward_queries(layer):
        if slow > 1:
            wait_for(qg.at[layer, pl.ds(0, slow - 1)], zr.at[layer])
            if fast > 1:
                for d in range(1, slow):
                    src = lax.rem(my_slow + d, slow) * fast + my_fast
                    block = qg.at[layer, src]
                    remote(block, block, ys.at[layer], yr.at[layer], partner).start()

    own_copy.wait()
    forward_queries(jnp.int32(0))

    def first_pass(layer):
        slot = lax.rem(layer, slots)
        queries = qg[layer].astype(jnp.float32).reshape(n * rows, HD)
        head = lax.rem(lax.broadcasted_iota(jnp.int32, (n * rows, HD), 0), heads)
        pieces = [
            jnp.where((head >= g * per_group) & (head < (g + 1) * per_group), queries, 0.0)
            for g in range(groups)
        ]
        spread_queries = jnp.concatenate(pieces, axis=1).astype(jnp.bfloat16)
        key_slot = lax.rem(layer, KEY_SLOTS)
        for c in range(0, key_count, SCORE_COLUMNS):
            w[slot, :, c : c + SCORE_COLUMNS] = lax.dot_general(
                spread_queries, kbuf[key_slot, c : c + SCORE_COLUMNS, :],
                (((1,), (1,)), ((), ())), preferred_element_type=jnp.float32,
            )
        limit = tokens - LAST - (me * key_count + key_count - LANES)

        def normalise(block, stats):
            maxima = []
            for u in range(BLOCK):
                i = block * BLOCK + u
                at = pl.ds(pl.multiple_of(i * heads, heads), heads)
                last = w[slot, at, key_count - LANES :]
                last = jnp.where(lane <= limit + i, last, -jnp.inf)
                w[slot, at, key_count - LANES :] = last
                top = last
                for t in range(tiles - 1):
                    top = jnp.maximum(top, w[slot, at, t * LANES : (t + 1) * LANES])
                maxima.append(jnp.max(top, axis=1, keepdims=True))
            for u in range(BLOCK):
                i = block * BLOCK + u
                at = pl.ds(pl.multiple_of(i * heads, heads), heads)
                top = jnp.broadcast_to(maxima[u], (heads, LANES))
                total = None
                for t in range(tiles):
                    cols = slice(t * LANES, (t + 1) * LANES)
                    weight = jnp.exp2((w[slot, at, cols] - top) * scale)
                    w[slot, at, cols] = weight
                    total = weight if total is None else total + weight
                total = jnp.sum(total, axis=1, keepdims=True)
                stats = jnp.where(lane == i, top, stats)
                stats = jnp.where(lane == LAST + i, total, stats)
            return stats

        st_tx[layer] = lax.fori_loop(
            0, LAST // BLOCK, normalise, jnp.zeros((heads, LANES), jnp.float32)
        )

    def shifted(before, now, steps):
        return jnp.where(lane < steps, before, now)

    def second_pass(layer):
        slot = lax.rem(layer, slots)
        if n > 1:
            wait_for(st_rx.at[layer, pl.ds(0, n - 1)], sr.at[layer])
        own = st_tx[layer]
        others = [st_rx[layer, lax.rem(me + d, n)] for d in range(1, n)]
        top = functools.reduce(jnp.maximum, others, own)
        mine = jnp.exp2((own - top) * scale)
        total = pltpu.roll(own, LAST, 1) * mine
        for other in others:
            total += pltpu.roll(other, LAST, 1) * jnp.exp2((other - top) * scale)
        factor = mine / total * ratio

        zero = jnp.zeros((heads, LANES), jnp.float32)
        for t in range(tiles):
            cols = slice(t * LANES, (t + 1) * LANES)
            vert_ref[layer, :, cols] = zero
            slash_ref[layer, :, cols] = zero
        ov_tx[layer] = zero

        def gather_block(block, factor):
            scales = [
                jnp.broadcast_to(factor[:, u : u + 1], (heads, LANES)) for u in range(BLOCK)
            ]
            before = {}
            for t in range(tiles + 1):
                cols = slice(t * LANES, (t + 1) * LANES)
                if t < tiles:
                    level = []
                    for u in range(BLOCK):
                        at = pl.ds(pl.multiple_of((block * BLOCK + u) * heads, heads), heads)
                        level.append(w[slot, at, cols] * scales[u])
                    vert_ref[layer, :, cols] += functools.reduce(jnp.add, level)
                else:
                    level = [None] * BLOCK
                steps = 1
                while len(level) > 1:
                    following = []
                    for a in range(0, len(level), 2):
                        now = zero if level[a] is None else pltpu.roll(level[a], steps, 1)
                        value = shifted(before.get((steps, a), zero), now, steps)
                        before[steps, a] = now
                        following.append(value if level[a + 1] is None else value + level[a + 1])
                    level = following
                    steps *= 2
                old = slash_ref[layer, :, cols] if t < tiles else ov_tx[layer]
                now = pltpu.roll(old, BLOCK, 1)
                value = shifted(before.get("acc", zero), now, BLOCK) + level[0]
                before["acc"] = now
                if t < tiles:
                    slash_ref[layer, :, cols] = value
                else:
                    ov_tx[layer] = value
            return pltpu.roll(factor, LANES - BLOCK, 1)

        lax.fori_loop(0, LAST // BLOCK, gather_block, factor)

    def send_stats(layer):
        for d in range(1, n):
            dest = lax.rem(me + d, n)
            remote(st_tx.at[layer], st_rx.at[layer, me], ss.at[layer], sr.at[layer], dest).start()

    def overflow_copy(layer):
        return remote(
            ov_tx.at[layer], ov_rx.at[layer], osem.at[layer], orsem.at[layer],
            lax.rem(me + 1, n),
        )

    def add_overflow(layer):
        @pl.when(me > 0)
        def _():
            overflow_copy(layer).wait_recv()
            slash_ref[layer, :, :LANES] += ov_rx[layer]

    def step(it, carry):
        @pl.when((it > LAG) & (it <= layers + LAG) & (me < n - 1))
        def _():
            overflow_copy(it - LAG - 1).start()

        @pl.when(it + 1 < layers)
        def _():
            forward_queries(it + 1)

        @pl.when(it < layers)
        def _():
            @pl.when(it + KEY_SLOTS - 1 < layers)
            def _():
                key_copy(it + KEY_SLOTS - 1).start()

            if fast > 1:
                wait_for(qg.at[it, pl.ds(0, slow)], yr.at[it])
            key_copy(it).wait()
            first_pass(it)

        @pl.when((it >= LAG) & (it < layers + LAG))
        def _():
            second_pass(it - LAG)

        @pl.when(it < layers)
        def _():
            send_stats(it)

        @pl.when(it >= LAG + 2)
        def _():
            add_overflow(it - LAG - 2)

        return carry

    lax.fori_loop(0, layers + LAG + 2, step, 0)

    def drain(layer, carry):
        if slow > 1:
            wait_for(qg.at[layer, pl.ds(0, slow - 1)], zs.at[layer])
        if fast > 1:
            wait_for(qg.at[layer, pl.ds(0, slow)], ys.at[layer])
        if n > 1:
            wait_for(st_rx.at[layer, pl.ds(0, n - 1)], ss.at[layer])

        @pl.when(me < n - 1)
        def _():
            overflow_copy(layer).wait_send()

        return carry

    lax.fori_loop(0, layers, drain, 0)


def on_device(n, fast, tail_queries, keys):
    layers, own_rows, width = tail_queries.shape
    heads = width // HD
    rows = own_rows * heads
    key_count = keys.shape[1]
    queries = tail_queries.reshape(layers, rows, HD)
    out = jax.ShapeDtypeStruct((layers, heads, key_count), jnp.float32)
    dma = pltpu.SemaphoreType.DMA
    return pl.pallas_call(
        functools.partial(kernel, n, fast),
        out_shape=(out, out),
        in_specs=[
            pl.BlockSpec(memory_space=pltpu.VMEM),
            pl.BlockSpec(memory_space=pl.ANY),
        ],
        out_specs=(
            pl.BlockSpec(memory_space=pltpu.VMEM),
            pl.BlockSpec(memory_space=pltpu.VMEM),
        ),
        scratch_shapes=[
            pltpu.VMEM((layers, n, rows, HD), jnp.bfloat16),
            pltpu.VMEM((KEY_SLOTS, key_count, keys.shape[2]), jnp.bfloat16),
            pltpu.VMEM((LAG + 1, LAST * heads, key_count), jnp.float32),
            pltpu.VMEM((layers, heads, LANES), jnp.float32),
            pltpu.VMEM((layers, n, heads, LANES), jnp.float32),
            pltpu.VMEM((layers, heads, LANES), jnp.float32),
            pltpu.VMEM((layers, heads, LANES), jnp.float32),
            dma, dma((KEY_SLOTS,)),
            dma((layers,)), dma((layers,)), dma((layers,)), dma((layers,)),
            dma((layers,)), dma((layers,)), dma((layers,)), dma((layers,)),
        ],
        compiler_params=pltpu.CompilerParams(
            collective_id=0, has_side_effects=True, vmem_limit_bytes=56 * 1024 * 1024
        ),
    )(queries, keys)


def solution(mesh):
    n = mesh.shape["seq"]
    fast = 2 if n % 2 == 0 else 1
    return jax.shard_map(
        functools.partial(on_device, n, fast),
        mesh=mesh,
        in_specs=(P(None, "seq", "head"), P(None, "seq", "head")),
        out_specs=(P(None, "head", "seq"), P(None, "head", "seq")),
        check_vma=False,
    )
```

time: 733 us -> 86.3 us (0.12); the launches traced: 724 us -> 85.8 us
  local copies, waits for them, and re-layouts: 474 us -> 5.6 us
  other arithmetic: 113 us -> 0 us
  Pallas kernels: 0 us -> 79.6 us
  blocking collectives: 68.7 us -> 0 us
  waiting for transfers between devices: 33.2 us -> 0 us
  matrix products: 18.1 us -> 0 us
  between operations: 14.1 us -> 0.64 us
    slice x122 -> x0, local copies, waits for them, and re-layouts: 251 us -> none  [the longest x60 136 us: diagonal_sums(): even_rows = rows[:, 0::2, :]]
    rev x10 -> x0, local copies, waits for them, and re-layouts: 102 us -> none  [diagonal_sums(): probabilities[:, ::-1, :]]
    pallas_call x0 -> x1, Pallas kernels: none -> 79.6 us  [on_device(): pl.pallas_call(functools.partial(kernel, n, fast), out_shape=(out, out),...]
    add x91 -> x0, other arithmetic: 52.6 us -> none  [the longest x50 51.7 us: diagonal_sums(): rows = even_rows + odd_rows]
    pad x10 -> x0, local copies, waits for them, and re-layouts: 47.2 us -> none  [diagonal_sums(): jnp.pad(probabilities[:, ::-1, :], ((0, 0), (0, 0), (0, width - key_count)))]
    dynamic_slice x40 -> x0, local copies, waits for them, and re-layouts: 44.4 us -> none  [on_device(): local_max, local_total, blocks = lax.map(first_pass, (gathered, keys))]
    pmax x1 -> x0, blocking collectives: 35.4 us -> none  [stats_every(): row_max = lax.pmax(local_max, 'seq')]
    psum x1 -> x0, blocking collectives: 33.4 us -> none  [stats_every(): row_total = lax.psum(local_total * jnp.exp(local_max - row_max), 'seq')]
  transfers between devices with their start and end apart: 2 -> 0, of which waited for: 1 -> 0; matrix products, arithmetic and copies ran while one was open for 2% -> 0% of each run, Pallas kernels for 0% -> 0%
where the time goes in v1:
time: 86.3 us; the launch traced here: 85.8 us
  Pallas kernels  79.6 us (92%)
  local copies, waits for them, and re-layouts  5.6 us (6%)
    pallas_call x1, Pallas kernels, on_device(): pl.pallas_call(functools.partial(kernel, n, fast), out_shape=(out, out),...  79.6 us
    unnamed x2, local copies, waits for them, and re-layouts  3.95 us

profile of v1, /device:TPU:0, one launch (start us, length us, event | category | flops | bytes accessed | tf_op | source)
XLA Modules:
  0.0 85.8 jit_solution(17909866971354541101)
XLA Ops:
  0.6 1.7 %reshape.7.q_ref = bf16[10,64,128]{2,1,0:T(8,128)(2,1)} reshape(bf16[10,8,1024]{2,1,0:T(8,128)(2,1)} %param.2) | data formatting | bytes 327680 | tf_op jit(solution)/shard_map/reshape | solution.py:275
  2.3 79.6 %shard_map.41 = (f32[10,8,2048]{2,1,0:T(8,128)}, f32[10,8,2048]{2,1,0:T(8,128)}) custom-call(bf16[10,64,128]{2,1,0:T(8,128)(2,1)} %reshape.7.q_ref, bf16[10,2048,256]{2,1,0:T(8,128)(2,1)} %k_ref.1), custom_call_target="tpu_custom_call" | custom-call | tf_op jit(solution)/shard_map/pallas_call | solution.py:278
  81.9 2.0 %copy.6 = f32[10,8,2048]{2,1,0:T(8,128)} copy(f32[10,8,2048]{2,1,0:T(8,128)} %get-tuple-element.4) | data formatting | bytes 1310720
  83.9 2.0 %copy.7 = f32[10,8,2048]{2,1,0:T(8,128)} copy(f32[10,8,2048]{2,1,0:T(8,128)} %get-tuple-element.5) | data formatting | bytes 1310720

commit v2 on v1

v2 whole, which is shorter than its diff:
```python
import functools
import math

import jax
import jax.numpy as jnp
from jax import lax
from jax.experimental import pallas as pl
from jax.experimental.pallas import tpu as pltpu
from jax.sharding import PartitionSpec as P

HD = 128
LAST = 64
LANES = 128
LAG = 4
KEY_SLOTS = 3
BLOCK = 8
BLOCKS = LAST // BLOCK
SLOTS = LAG + 1


def kernel(
    n, fast, q_ref, k_ref, vert_ref, slash_ref,
    qg, kbuf, qx, tops, totals, raw, w, st_tx, st_rx, ov_tx, ov_rx,
    own_sem, k_sem, zs, zr, ys, yr, ss, sr, osem, orsem,
):
    layers, rows, _ = q_ref.shape
    key_count = k_ref.shape[1]
    groups = k_ref.shape[2] // HD
    heads = rows * n // LAST
    per_group = heads // groups
    tiles = key_count // LANES
    slow = n // fast
    tokens = key_count * n
    scale = math.log2(math.e) / math.sqrt(HD)
    ratio = tokens / LAST

    me = lax.axis_index("seq")
    my_slow = lax.div(me, fast)
    my_fast = lax.rem(me, fast)
    lane = lax.broadcasted_iota(jnp.int32, (heads, LANES), 1)

    def remote(src, dst, send, recv, dest):
        return pltpu.make_async_remote_copy(
            src_ref=src, dst_ref=dst, send_sem=send, recv_sem=recv,
            device_id={"seq": dest}, device_id_type=pl.DeviceIdType.MESH,
        )

    def wait_for(ref, sem):
        pltpu.make_async_copy(ref, ref, sem).wait()

    def key_copy(layer):
        slot = layer % KEY_SLOTS
        return pltpu.make_async_copy(k_ref.at[layer], kbuf.at[slot], k_sem.at[slot])

    for layer in range(min(KEY_SLOTS - 1, layers)):
        key_copy(layer).start()
    own_copy = pltpu.make_async_copy(q_ref, qg.at[:, me], own_sem)
    own_copy.start()

    barrier = pltpu.get_barrier_semaphore()
    for d in range(1, n):
        pl.semaphore_signal(
            barrier, inc=1, device_id={"seq": lax.rem(me + d, n)},
            device_id_type=pl.DeviceIdType.MESH,
        )
    pl.semaphore_wait(barrier, n - 1)

    partner = my_slow * fast + lax.rem(my_fast + 1, fast)

    def send_queries(layer, carry):
        for d in range(1, slow):
            dest = lax.rem(my_slow + d, slow) * fast + my_fast
            remote(q_ref.at[layer], qg.at[layer, me], zs.at[layer], zr.at[layer], dest).start()
        if fast > 1:
            remote(q_ref.at[layer], qg.at[layer, me], ys.at[layer], yr.at[layer], partner).start()
        return carry

    lax.fori_loop(0, layers, send_queries, 0)

    def forward_queries(layer):
        if slow > 1:
            wait_for(qg.at[layer, pl.ds(0, slow - 1)], zr.at[layer])
            if fast > 1:
                for d in range(1, slow):
                    src = lax.rem(my_slow + d, slow) * fast + my_fast
                    block = qg.at[layer, src]
                    remote(block, block, ys.at[layer], yr.at[layer], partner).start()

    own_copy.wait()
    forward_queries(0)

    limit = tokens - LAST - (me * key_count + key_count - LANES)
    last_tile = tiles - 1

    def spread_queries(layer):
        queries = qg[layer].astype(jnp.float32).reshape(n * rows, HD)
        head = lax.rem(lax.broadcasted_iota(jnp.int32, (n * rows, HD), 0), heads)
        pieces = [
            jnp.where((head >= g * per_group) & (head < (g + 1) * per_group), queries, 0.0)
            for g in range(groups)
        ]
        qx[...] = jnp.concatenate(pieces, axis=1).astype(jnp.bfloat16)

    def block_rows(block, u):
        return pl.ds(pl.multiple_of((block * BLOCK + u) * heads, heads), heads)

    def score_block(layer, block):
        width = key_count // BLOCKS
        at = pl.ds(pl.multiple_of(block * width, width), width)
        raw[layer % 2][:, at] = lax.dot_general(
            qx[...], kbuf[layer % KEY_SLOTS, at, :],
            (((1,), (1,)), ((), ())), preferred_element_type=jnp.float32,
        )

    def load_score(layer, block, u, t):
        value = raw[layer % 2][block_rows(block, u), t * LANES : (t + 1) * LANES]
        if t == last_tile:
            value = jnp.where(lane <= limit + block * BLOCK + u, value, -jnp.inf)
        return value

    def row_top(layer, block, u, stats):
        top = load_score(layer, block, u, 0)
        for t in range(1, tiles):
            top = jnp.maximum(top, load_score(layer, block, u, t))
        top = jnp.broadcast_to(jnp.max(top, axis=1, keepdims=True), (heads, LANES))
        tops[u] = top
        return jnp.where(lane == block * BLOCK + u, top, stats)

    def row_weights(layer, block, u, top):
        at = block_rows(block, u)
        sums = [None] * 2
        for t in range(tiles):
            weight = jnp.exp2((load_score(layer, block, u, t) - top) * scale)
            w[layer % SLOTS][at, t * LANES : (t + 1) * LANES] = weight
            sums[t % 2] = weight if sums[t % 2] is None else sums[t % 2] + weight
        totals[u] = sums[0] + sums[1]

    def row_total(block, u, total, stats):
        total = jnp.sum(total, axis=1, keepdims=True)
        return jnp.where(lane == LAST + block * BLOCK + u, total, stats)

    def shifted(before, now, steps):
        return jnp.where(lane < steps, before, now)

    def factors(layer):
        if n > 1:
            wait_for(st_rx.at[layer, pl.ds(0, n - 1)], sr.at[layer])
        own = st_tx[layer]
        others = [st_rx[layer, lax.rem(me + d, n)] for d in range(1, n)]
        top = functools.reduce(jnp.maximum, others, own)
        mine = jnp.exp2((own - top) * scale)
        total = pltpu.roll(own, LAST, 1) * mine
        for other in others:
            total += pltpu.roll(other, LAST, 1) * jnp.exp2((other - top) * scale)
        return mine / total * ratio

    zero = jnp.zeros((heads, LANES), jnp.float32)

    def clear_sums(layer):
        for t in range(tiles):
            cols = slice(t * LANES, (t + 1) * LANES)
            vert_ref[layer, :, cols] = zero
            slash_ref[layer, :, cols] = zero
        ov_tx[layer] = zero

    def tree_sum(values):
        while len(values) > 1:
            pairs = [a + b for a, b in zip(values[::2], values[1::2])]
            values = pairs + values[len(pairs) * 2 :]
        return values[0]

    def sum_tile(layer, block, t, scales, before):
        cols = slice(t * LANES, (t + 1) * LANES)
        if t < tiles:
            level = [
                w[layer % SLOTS][block_rows(block, u), cols] * scales[u] for u in range(BLOCK)
            ]
            vert_ref[layer, :, cols] += tree_sum(level)
        moved = []
        for u in range(BLOCK - 1):
            steps = BLOCK - 1 - u
            now = zero if t == tiles else pltpu.roll(level[u], steps, 1)
            moved.append(shifted(before.get(u, zero), now, steps))
            before[u] = now
        if t < tiles:
            moved.append(level[-1])
        moved = tree_sum(moved)
        old = slash_ref[layer, :, cols] if t < tiles else ov_tx[layer]
        now = pltpu.roll(old, BLOCK, 1)
        value = shifted(before.get("acc", zero), now, BLOCK) + moved
        before["acc"] = now
        if t < tiles:
            slash_ref[layer, :, cols] = value
        else:
            ov_tx[layer] = value

    def compute(score, weigh, gather):
        factor = first_stats = zero
        if score is not None:
            spread_queries(score)
        if weigh is not None:
            for u in range(BLOCK):
                first_stats = row_top(weigh, 0, u, first_stats)
                totals[u] = zero
        if gather is not None:
            factor = factors(gather)
            clear_sums(gather)

        def body(block, carry):
            stats, factor = carry
            scales = [
                jnp.broadcast_to(factor[:, u : u + 1], (heads, LANES)) for u in range(BLOCK)
            ] if gather is not None else None
            before = {}
            if weigh is not None:
                old_tops = [tops[u] for u in range(BLOCK)]
                old_totals = [totals[u] for u in range(BLOCK)]
                following = lax.rem(block + 1, BLOCKS)
                for u in range(BLOCK):
                    kept = row_total(block - 1, u, old_totals[u], stats)
                    stats = jnp.where(block > 0, kept, stats)
            if score is not None:
                score_block(score, block)
            done = 0
            for u in range(BLOCK):
                if weigh is not None:
                    stats = row_top(weigh, following, u, stats)
                    row_weights(weigh, block, u, old_tops[u])
                if gather is not None:
                    until = (tiles + 1) * (u + 1) // BLOCK
                    for t in range(done, until):
                        sum_tile(gather, block, t, scales, before)
                    done = until
            if gather is not None:
                factor = pltpu.roll(factor, LANES - BLOCK, 1)
            return stats, factor

        stats, _ = lax.fori_loop(0, BLOCKS, body, (first_stats, factor))
        if weigh is not None:
            for u in range(BLOCK):
                stats = row_total(BLOCKS - 1, u, totals[u], stats)
            st_tx[weigh] = stats

    def send_stats(layer):
        for d in range(1, n):
            dest = lax.rem(me + d, n)
            remote(st_tx.at[layer], st_rx.at[layer, me], ss.at[layer], sr.at[layer], dest).start()

    def overflow_copy(layer):
        return remote(
            ov_tx.at[layer], ov_rx.at[layer], osem.at[layer], orsem.at[layer],
            lax.rem(me + 1, n),
        )

    def add_overflow(layer):
        @pl.when(me > 0)
        def _():
            overflow_copy(layer).wait_recv()
            slash_ref[layer, :, :LANES] += ov_rx[layer]

    def send_overflow(layer):
        @pl.when(me < n - 1)
        def _():
            overflow_copy(layer).start()

    def within(layer):
        return layer if 0 <= layer < layers else None

    for it in range(layers + LAG):
        score, weigh, gather = within(it), within(it - 1), within(it - LAG)
        if within(it + 1) is not None:
            forward_queries(it + 1)
        if score is not None:
            if it + KEY_SLOTS - 1 < layers:
                key_copy(it + KEY_SLOTS - 1).start()
            if fast > 1:
                wait_for(qg.at[it, pl.ds(0, slow)], yr.at[it])
            key_copy(it).wait()
        compute(score, weigh, gather)
        if gather is not None:
            send_overflow(gather)
        if weigh is not None:
            send_stats(weigh)
        if within(gather - 2 if gather is not None else -1) is not None:
            add_overflow(gather - 2)
    for layer in range(max(layers - 2, 0), layers):
        add_overflow(layer)

    def drain(layer, carry):
        if slow > 1:
            wait_for(qg.at[layer, pl.ds(0, slow - 1)], zs.at[layer])
        if fast > 1:
            wait_for(qg.at[layer, pl.ds(0, slow)], ys.at[layer])
        if n > 1:
            wait_for(st_rx.at[layer, pl.ds(0, n - 1)], ss.at[layer])

        @pl.when(me < n - 1)
        def _():
            overflow_copy(layer).wait_send()

        return carry

    lax.fori_loop(0, layers, drain, 0)


def on_device(n, fast, tail_queries, keys):
    layers, own_rows, width = tail_queries.shape
    heads = width // HD
    rows = own_rows * heads
    key_count = keys.shape[1]
    queries = tail_queries.reshape(layers, rows, HD)
    out = jax.ShapeDtypeStruct((layers, heads, key_count), jnp.float32)
    dma = pltpu.SemaphoreType.DMA
    return pl.pallas_call(
        functools.partial(kernel, n, fast),
        out_shape=(out, out),
        in_specs=[
            pl.BlockSpec(memory_space=pltpu.VMEM),
            pl.BlockSpec(memory_space=pl.ANY),
        ],
        out_specs=(
            pl.BlockSpec(memory_space=pltpu.VMEM),
            pl.BlockSpec(memory_space=pltpu.VMEM),
        ),
        scratch_shapes=[
            pltpu.VMEM((layers, n, rows, HD), jnp.bfloat16),
            pltpu.VMEM((KEY_SLOTS, key_count, keys.shape[2]), jnp.bfloat16),
            pltpu.VMEM((LAST * heads, keys.shape[2]), jnp.bfloat16),
            pltpu.VMEM((BLOCK, heads, LANES), jnp.float32),
            pltpu.VMEM((BLOCK, heads, LANES), jnp.float32),
            [pltpu.VMEM((LAST * heads, key_count), jnp.float32)] * 2,
            [pltpu.VMEM((LAST * heads, key_count), jnp.float32)] * SLOTS,
            pltpu.VMEM((layers, heads, LANES), jnp.float32),
            pltpu.VMEM((layers, n, heads, LANES), jnp.float32),
            pltpu.VMEM((layers, heads, LANES), jnp.float32),
            pltpu.VMEM((layers, heads, LANES), jnp.float32),
            dma, dma((KEY_SLOTS,)),
            dma((layers,)), dma((layers,)), dma((layers,)), dma((layers,)),
            dma((layers,)), dma((layers,)), dma((layers,)), dma((layers,)),
        ],
        compiler_params=pltpu.CompilerParams(
            collective_id=0, has_side_effects=True, vmem_limit_bytes=56 * 1024 * 1024
        ),
    )(queries, keys)


def solution(mesh):
    n = mesh.shape["seq"]
    fast = 2 if n % 2 == 0 else 1
    return jax.shard_map(
        functools.partial(on_device, n, fast),
        mesh=mesh,
        in_specs=(P(None, "seq", "head"), P(None, "seq", "head")),
        out_specs=(P(None, "head", "seq"), P(None, "head", "seq")),
        check_vma=False,
    )
```

time: 86.3 us -> 67.8 us (0.79)
  Pallas kernels: 79.6 us -> 61.4 us
    pallas_call x1, Pallas kernels: 79.6 us -> 61.4 us  [on_device(): pl.pallas_call(functools.partial(kernel, n, fast), out_shape=(out, out),...]
where the time goes in v2:
time: 67.8 us; the launch traced here: 67.6 us
  Pallas kernels  61.4 us (91%)
  local copies, waits for them, and re-layouts  5.6 us (8%)
    pallas_call x1, Pallas kernels, on_device(): pl.pallas_call(functools.partial(kernel, n, fast), out_shape=(out, out),...  61.4 us
    unnamed x2, local copies, waits for them, and re-layouts  3.95 us
    reshape x1, local copies, waits for them, and re-layouts, on_device(): queries = tail_queries.reshape(layers, rows, HD)  1.66 us

profile of v2, /device:TPU:0, one launch (start us, length us, event | category | flops | bytes accessed | tf_op | source)
XLA Modules:
  0.0 67.6 jit_solution(11850917274217618074)
XLA Ops:
  0.6 1.7 %reshape.7.q_ref = bf16[10,64,128]{2,1,0:T(8,128)(2,1)} reshape(bf16[10,8,1024]{2,1,0:T(8,128)(2,1)} %param.2) | data formatting | bytes 327680 | tf_op jit(solution)/shard_map/reshape | solution.py:311
  2.3 61.4 %shard_map.41 = (f32[10,8,2048]{2,1,0:T(8,128)}, f32[10,8,2048]{2,1,0:T(8,128)}) custom-call(bf16[10,64,128]{2,1,0:T(8,128)(2,1)} %reshape.7.q_ref, bf16[10,2048,256]{2,1,0:T(8,128)(2,1)} %k_ref.1), custom_call_target="tpu_custom_call" | custom-call | tf_op jit(solution)/shard_map/pallas_call | solution.py:314
  63.7 2.0 %copy.6 = f32[10,8,2048]{2,1,0:T(8,128)} copy(f32[10,8,2048]{2,1,0:T(8,128)} %get-tuple-element.4) | data formatting | bytes 1310720
  65.6 2.0 %copy.7 = f32[10,8,2048]{2,1,0:T(8,128)} copy(f32[10,8,2048]{2,1,0:T(8,128)} %get-tuple-element.5) | data formatting | bytes 1310720
